TPU v7x, 128 devices: a whole 4x4x4 slice. The times are simulated.
128 devices in a mesh: dp: 32 (over x, y, core), group: 4 (over z).
Axes of the slice: x: 4, y: 4, z: 4, core: 2. Of those that a mesh axis runs over, the one named last changes fastest.
Arguments:
- images: bfloat16 [16384, 512], P(('dp', 'group')), may hold values from -1 to 1
- texts: bfloat16 [16384, 512], P(('dp', 'group')), may hold values from -1 to 1
- log_scale: float32 [], replicated, may hold values from 2 to 2.7
Outputs:
- grad_images: bfloat16 [16384, 512], P(('dp', 'group'))
- grad_texts: bfloat16 [16384, 512], P(('dp', 'group'))
- loss: float32 [], replicated
- grad_scale: float32 [], replicated
All inputs are finite; a program needn't handle non-finite values.
Results may differ from a plain program's by a relative error of at most 0.0013.
The roundings to bfloat16 on the way count: a program that leaves them out, or rounds other values in their place, can miss the bound.
Values may be sent and summed in bfloat16 or wider, within the bound.
No kernel may reach another device: no remote copies, remote signals or barrier semaphores. Data moves between devices by JAX's collectives and lax.ppermute only.
A program may use at most 128 MiB of HBM per device.

v0:
```python
import jax
import jax.numpy as jnp
from jax import lax
from jax.sharding import Mesh
from jax.sharding import PartitionSpec as P

DP_GROUP = ("dp_0", "dp_1", "dp_2", "group")


def in_one_piece(arrays, axis, split_dim, concat_dim, along):
    ends, at = ([], 0)
    for a in arrays[:-1]:
        at += a.shape[along]
        ends.append(at)
    both = jnp.concatenate(arrays, axis=along)
    return tuple(
        jnp.split(
            lax.all_to_all(both, axis, split_axis=split_dim, concat_axis=concat_dim, tiled=True),
            ends,
            axis=along,
        )
    )


def rows_first(arrays, axis, dims):
    turned = [jnp.moveaxis(a, dim, 0) for a, dim in zip(arrays, dims)]
    both = jnp.concatenate([t.reshape(len(t), -1) for t in turned], axis=1)
    filled, at, outs = (lax.all_gather(both, axis, axis=0, tiled=True), 0, [])
    for t, dim in zip(turned, dims):
        share = filled[:, at : at + t[0].size].reshape(-1, *t.shape[1:])
        outs.append(jnp.moveaxis(share, 0, dim))
        at += t[0].size
    return tuple(outs)


def one_axis_at_a_time(value, axes):
    for axis in axes:
        value = lax.psum(value, axis)
    return value


def body(images, texts, log_scale):
    row_count = images.shape[0]
    device_count = lax.axis_size(DP_GROUP)
    pair_total = row_count * device_count
    texts_whole = lax.all_gather(texts, DP_GROUP, axis=0, tiled=True)
    images_whole = lax.all_gather(images, DP_GROUP, axis=0, tiled=True)
    logit_scale = jnp.exp(log_scale)
    first_pair = lax.axis_index(DP_GROUP) * row_count
    contract_last = (((1,), (1,)), ((), ()))
    contract_first = (((0,), (0,)), ((), ()))
    row_logits = logit_scale * lax.dot_general(
        images, texts_whole, contract_last, preferred_element_type=jnp.float32
    )
    row_top = jnp.max(row_logits, axis=1)
    row_lse = row_top + jnp.log(jnp.sum(jnp.exp(row_logits - row_top[:, None]), axis=1))
    paired = jnp.diagonal(lax.dynamic_slice_in_dim(row_logits, first_pair, row_count, 1))
    part_top = jnp.max(row_logits, axis=0)
    part_sum = jnp.sum(jnp.exp(row_logits - part_top[None, :]), axis=0)
    got_top, got_sum = in_one_piece(
        (part_top.reshape(device_count, row_count), part_sum.reshape(device_count, row_count)),
        DP_GROUP,
        0,
        0,
        1,
    )
    col_top = jnp.max(got_top, axis=0)
    col_lse = col_top + jnp.log(jnp.sum(got_sum * jnp.exp(got_top - col_top[None, :]), axis=0))
    row_whole, col_whole = rows_first((row_lse, col_lse), DP_GROUP, (0, 0))
    own_pairs = (
        jnp.arange(pair_total)[None, :] == (first_pair + jnp.arange(row_count))[:, None]
    ).astype(jnp.float32)
    row_grad = (
        0.5 * (jnp.exp(row_logits - row_lse[:, None]) + jnp.exp(row_logits - col_whole[None, :]))
        - own_pairs
    )
    scale_part = jnp.sum(row_grad * row_logits)
    row_weights = row_grad.astype(jnp.bfloat16)
    grad_images = (
        logit_scale * jnp.dot(row_weights, texts_whole, preferred_element_type=jnp.float32)
    ).astype(jnp.bfloat16)
    col_logits = logit_scale * lax.dot_general(
        images_whole, texts, contract_last, preferred_element_type=jnp.float32
    )
    col_grad = (
        0.5 * (jnp.exp(col_logits - row_whole[:, None]) + jnp.exp(col_logits - col_lse[None, :]))
        - own_pairs.T
    )
    text_sum = logit_scale * lax.dot_general(
        col_grad.astype(jnp.bfloat16),
        images_whole,
        contract_first,
        preferred_element_type=jnp.float32,
    )
    grad_texts = text_sum.astype(jnp.bfloat16)
    loss_part = jnp.sum(row_lse) + jnp.sum(col_lse) - 2.0 * jnp.sum(paired)
    loss_total, scale_total = (
        one_axis_at_a_time(loss_part, DP_GROUP),
        one_axis_at_a_time(scale_part, DP_GROUP),
    )
    return (grad_images, grad_texts, loss_total / (2.0 * pair_total), scale_total / pair_total)


def solution(mesh):
    split = Mesh(
        mesh.devices.reshape(4, 4, 2, mesh.shape["group"]), ("dp_0", "dp_1", "dp_2", "group")
    )
    placed = (P(DP_GROUP, None), P(DP_GROUP, None), P())
    return jax.shard_map(
        body,
        mesh=split,
        in_specs=placed,
        out_specs=(P(DP_GROUP, None), P(DP_GROUP, None), P(), P()),
        check_vma=False,
    )
```

profile of v0, /device:TPU:0, one launch (start us, length us, event | category | flops | bytes accessed | tf_op | source)
XLA Modules:
  0.0 263.8 jit_solution(17786985613269034500)
XLA Ops:
  7.2 0.0 all-gather.3.cloned.1.call-start
  7.2 0.7 all-gather.3.cloned.1.call-update
  7.9 0.0 all-gather.5.cloned.1.call-start
  7.9 0.7 all-gather.5.cloned.1.call-update
  9.4 84.2 %all-gather.3.cloned.1.call-done = bf16[16384,512]{1,0:T(8,128)(2,1)} async-done(((bf16[128,512]{1,0:T(8,128)(2,1)}), bf16[16384,512]{1,0:T(8,128)(2,1)}) %all-gather.3.cloned.1.call-update) | async-done | bytes 16777232 | tf_op jit(solution)/shard_map/all_gather | solution.py:46
  93.6 14.5 %fusion.19 = (f32[128]{0:T(128)S(1)}, f32[16384]{0:T(1024)S(1)}, f32[128,16384]{1,0:T(8,128)}) fusion(bf16[128,512]{1,0:T(8,128)(2,1)} %param.3, bf16[16384,512]{1,0:T(8,128)(2,1)} %all-gather.3.cloned.1.call-done, f32[]{:T(128)S(6)} %exp.24), kind=kOutput, calls=%fused_computation.34 | convolution fusion | flops 2153758720 | bytes 25362948 | tf_op jit(solution)/shard_map/dot_general | solution.py:52
  108.1 4.7 %exponential_reduce_fusion.1 = (f32[128]{0:T(128)S(1)}, f32[16384]{0:T(1024)S(1)}) fusion(f32[128,16384]{1,0:T(8,128)} %get-tuple-element.22, f32[128]{0:T(128)S(1)} %get-tuple-element.6, f32[16384]{0:T(1024)S(1)} %get-tuple-element.7), kind=kLoop, calls=%fused_computation.9 | loop fusion | flops 8372096 | bytes 8520704 | tf_op jit(solution)/shard_map/reduce_sum | solution.py:56
  112.9 0.7 all_to_all.8
  113.6 8.2 %all-to-all-start = ((f32[128,1,256]{2,1,0:T(1,128)}), f32[128,1,256]{2,1,0:T(1,128)S(1)}, u32[]{:S(2)}, u32[]{:S(2)}) async-start(f32[128,1,256]{2,1,0:T(1,128)} %all_to_all.8), calls=%async_computation | async-start | bytes 262144 | tf_op jit(solution)/shard_map/all_to_all | solution.py:18
  121.9 0.9 constant_dynamic-slice_fusion
  122.7 1.2 gather_fusion
  124.0 0.6 reduce_sum.68
  125.2 0.6 fusion.21
  125.8 5.2 %all-to-all-done = f32[128,1,256]{2,1,0:T(1,128)S(1)} async-done(((f32[128,1,256]{2,1,0:T(1,128)}), f32[128,1,256]{2,1,0:T(1,128)S(1)}, u32[]{:S(2)}, u32[]{:S(2)}) %all-to-all-start) | async-done | bytes 131104 | tf_op jit(solution)/shard_map/all_to_all | solution.py:18
  131.1 0.6 fusion.20
  133.1 50.5 %all_gather.10 = f32[16384,2]{0,1:T(2,128)S(1)} all-gather(f32[128,2]{0,1:T(2,128)S(1)} %pad_maximum_fusion.1), channel_id=1, replica_groups=mesh['dp_0'=4,'dp_1'=4,'dp_2'=2,'group'=4] {'dp_0','dp_1','dp_2','group'}, dimensions={0}, use_global_device_ids=true | all-gather | bytes 132096 | tf_op jit(solution)/shard_map/all_gather | solution.py:28
  183.6 0.1 fusion.22
  183.7 6.5 %multiply_reduce_fusion = f32[]{:T(128)} fusion(f32[128,16384]{1,0:T(8,128)} %get-tuple-element.22, s32[128]{0:T(128)S(1)} %iota_add_fusion, f32[16384]{0:T(1024)S(1)} %bitcast.20, f32[128]{0:T(128)S(1)} %get-tuple-element.19), kind=kLoop, calls=%fused_computation.3 | loop fusion | flops 18874368 | bytes 8455172 | tf_op jit(solution)/shard_map/reduce_sum | solution.py:77
  190.2 10.4 %all-reduce.2 = (f32[]{:T(128)}, f32[]{:T(128)}) all-reduce(f32[]{:T(128)S(6)} %sub.87, f32[]{:T(128)} %multiply_reduce_fusion), channel_id=1, replica_groups=mesh['dp_0'=4,'dp_1'=4,'dp_2'=2,'group'=4] {'dp_0'}, use_global_device_ids=true, to_apply=%region_9.10 | all-reduce | flops 2 | bytes 16 | tf_op jit(solution)/shard_map/psum | solution.py:38
  200.6 8.8 %all-reduce.1 = (f32[]{:T(128)}, f32[]{:T(128)}) all-reduce(f32[]{:T(128)} %get-tuple-element.12, f32[]{:T(128)} %get-tuple-element.13), channel_id=1, replica_groups=mesh['dp_0'=4,'dp_1'=4,'dp_2'=2,'group'=4] {'dp_1'}, use_global_device_ids=true, to_apply=%region_10.11 | all-reduce | flops 2 | bytes 16 | tf_op jit(solution)/shard_map/psum | solution.py:38
  209.3 3.1 %all-reduce.3 = (f32[]{:T(128)}, f32[]{:T(128)}) all-reduce(f32[]{:T(128)} %get-tuple-element.10, f32[]{:T(128)} %get-tuple-element.11), channel_id=1, replica_groups=mesh['dp_0'=4,'dp_1'=4,'dp_2'=2,'group'=4] {'dp_2'}, use_global_device_ids=true, to_apply=%region_11.12 | all-reduce | flops 2 | bytes 16 | tf_op jit(solution)/shard_map/psum | solution.py:38
  212.4 10.0 %all-reduce = (f32[]{:T(128)}, f32[]{:T(128)}) all-reduce(f32[]{:T(128)} %get-tuple-element.14, f32[]{:T(128)} %get-tuple-element.15), channel_id=1, replica_groups=mesh['dp_0'=4,'dp_1'=4,'dp_2'=2,'group'=4] {'group'}, use_global_device_ids=true, to_apply=%region_12.13 | all-reduce | flops 2 | bytes 16 | tf_op jit(solution)/shard_map/psum | solution.py:38
  223.8 12.4 %fusion.12 = bf16[128,512]{1,0:T(8,128)(2,1)} fusion(bf16[16384,512]{1,0:T(8,128)(2,1)} %all-gather.3.cloned.1.call-done, f32[128,16384]{1,0:T(8,128)} %get-tuple-element.22, s32[128]{0:T(128)S(1)} %iota_add_fusion, f32[16384]{0:T(1024)S(1)} %bitcast.21, f32[128]{0:T(128)S(1)} %get-tuple-element.19, f32[]{:T(128)S(6)} %exp.24), kind=kOutput, calls=%fused_computation.19 | convolution fusion | flops 2164391936 | bytes 25363460 | tf_op jit(solution)/shard_map/dot_general | solution.py:80
  236.2 18.5 %fusion.15 = bf16[128,512]{1,0:T(8,128)(2,1)} fusion(bf16[16384,512]{1,0:T(8,128)(2,1)} %all-gather.5.cloned.1.call-done, bf16[128,512]{1,0:T(8,128)(2,1)S(1)} %copy-done, s32[128]{0:T(128)S(1)} %iota_add_fusion, f32[128]{0:T(128)S(1)} %get-tuple-element.17, f32[16384]{0:T(1024)S(1)} %bitcast.23, f32[]{:T(128)S(6)} %exp.24), kind=kOutput, calls=%fused_computation.20 | convolution fusion | flops 4313972736 | bytes 17105924 | tf_op jit(solution)/shard_map/dot_general | solution.py:89
  (10 shorter events, 0.1 us)
Async XLA Ops:
  7.2 86.4 %all-gather.3.cloned.1.call-start = ((), (), s32[]{:S(2)}) async-start(), calls=%async_computation.1 | async-start | bytes 16908288 | tf_op jit(solution)/shard_map/all_gather | solution.py:46
  7.9 228.3 %all-gather.5.cloned.1.call-start = ((), (), s32[]{:S(2)}) async-start(), calls=%async_computation.2 | async-start | bytes 16908288 | tf_op jit(solution)/shard_map/all_gather | solution.py:47
  113.6 17.4 %all-to-all-start = ((f32[128,1,256]{2,1,0:T(1,128)}), f32[128,1,256]{2,1,0:T(1,128)S(1)}, u32[]{:S(2)}, u32[]{:S(2)}) async-start(f32[128,1,256]{2,1,0:T(1,128)} %all_to_all.8), calls=%async_computation | async-start | bytes 262144 | tf_op jit(solution)/shard_map/all_to_all | solution.py:18
  223.8 12.4 %copy-start = (bf16[128,512]{1,0:T(8,128)(2,1)S(1)}, bf16[128,512]{1,0:T(8,128)(2,1)}, u32[]{:S(2)}) copy-start(bf16[128,512]{1,0:T(8,128)(2,1)} %param.4) | copy-start | bytes 393220
Sparse Core Ops, SparseCore 0:
  11.1 82.4 all-gather.2
  96.7 79.5 all-gather.4
where the time goes:
time: 264 us
  waiting for transfers between devices  90.8 us (34%)
  blocking collectives  82.8 us (31%)
  matrix products  45.4 us (17%)
  between operations  20.3 us (8%)
  other arithmetic  13.2 us (5%)
  starting transfers between devices  8.3 us (3%)
  local copies, waits for them, and re-layouts  2.96 us (1%)
    all_gather x1, waiting for transfers between devices, body(): texts_whole = lax.all_gather(texts, DP_GROUP, axis=0, tiled=True)  84.2 us
    all_gather x1, blocking collectives, rows_first(): filled, at, outs = (lax.all_gather(both, axis, axis=0, tiled=True), 0, [])  50.5 us
    psum x4, blocking collectives, one_axis_at_a_time(): value = lax.psum(value, axis)  32.3 us
    dot_general x1, matrix products, body(): lax.dot_general(col_grad.astype(jnp.bfloat16), images_whole, contract_fir...  18.5 us
    dot_general x1, matrix products, body(): lax.dot_general(images, texts_whole, contract_last, preferred_element_typ...  14.5 us
    dot_general x1, matrix products, body(): jnp.dot(row_weights, texts_whole, preferred_element_type=jnp.float32)  12.4 us
    all_to_all x1, starting transfers between devices, in_one_piece(): lax.all_to_all(both, axis, split_axis=split_dim, concat_axis=concat_dim,...  8.23 us
    reduce_sum x1, other arithmetic, body(): scale_part = jnp.sum(row_grad * row_logits)  6.49 us
  transfers between devices with their start and end apart: 3, of which 2 were waited for; matrix products, arithmetic and copies ran while one was open for 16% of the time, Pallas kernels for 0%

commit v1 on v0

--- a/solution.py
+++ b/solution.py
@@ -35,7 +35,7 @@
 
 def one_axis_at_a_time(value, axes):
     for axis in axes:
-        value = lax.psum(value, axis)
+        value = jnp.sum(lax.all_gather(value, axis), axis=0)
     return value
 
 

time: 264 us -> 279 us (1.057)
  local copies, waits for them, and re-layouts: 2.96 us -> 16.5 us
  other arithmetic: 13.2 us -> 18 us
    psum x4 -> x0, blocking collectives: 32.3 us -> none  [one_axis_at_a_time(): value = lax.psum(value, axis)]
    unnamed x0 -> x4, blocking collectives: none -> 29.9 us
    unnamed x3 -> x29, local copies, waits for them, and re-layouts: 0.02 us -> 13.6 us
    reduce_sum x0 -> x8, other arithmetic: none -> 4.81 us  [one_axis_at_a_time(): value = jnp.sum(lax.all_gather(value, axis), axis=0)]
  transfers between devices with their start and end apart: 3 -> 3, of which waited for: 2 -> 2; matrix products, arithmetic and copies ran while one was open for 16% -> 22% of each run, Pallas kernels for 0% -> 0%
where the time goes in v1:
time: 279 us; the launch traced here: 278 us
  waiting for transfers between devices  89.6 us (32%)
  blocking collectives  80.1 us (29%)
  matrix products  45.4 us (16%)
  between operations  20.3 us (7%)
  other arithmetic  18 us (6%)
  local copies, waits for them, and re-layouts  16.5 us (6%)
  starting transfers between devices  8.31 us (3%)
    all_gather x1, waiting for transfers between devices, body(): texts_whole = lax.all_gather(texts, DP_GROUP, axis=0, tiled=True)  83 us
    all_gather x1, blocking collectives, rows_first(): filled, at, outs = (lax.all_gather(both, axis, axis=0, tiled=True), 0, [])  50.3 us
    unnamed x4, blocking collectives  29.9 us
    dot_general x1, matrix products, body(): lax.dot_general(col_grad.astype(jnp.bfloat16), images_whole, contract_fir...  18.5 us
    dot_general x1, matrix products, body(): lax.dot_general(images, texts_whole, contract_last, preferred_element_typ...  14.5 us
    unnamed x29, local copies, waits for them, and re-layouts  13.6 us
    dot_general x1, matrix products, body(): jnp.dot(row_weights, texts_whole, preferred_element_type=jnp.float32)  12.4 us
    all_to_all x1, starting transfers between devices, in_one_piece(): lax.all_to_all(both, axis, split_axis=split_dim, concat_axis=concat_dim,...  8.23 us
  transfers between devices with their start and end apart: 3, of which 2 were waited for; matrix products, arithmetic and copies ran while one was open for 22% of the time, Pallas kernels for 0%

profile of v1, /device:TPU:0, one launch (start us, length us, event | category | flops | bytes accessed | tf_op | source)
XLA Modules:
  0.0 278.4 jit_solution(8413827872241767801)
XLA Ops:
  9.3 1.2 dynamic-slice
  10.6 83.0 %all-gather.3.cloned.1.call-done = bf16[16384,512]{1,0:T(8,128)(2,1)} async-done(((bf16[128,512]{1,0:T(8,128)(2,1)}), bf16[16384,512]{1,0:T(8,128)(2,1)}) %all-gather.3.cloned.1.call-update) | async-done | bytes 16777232 | tf_op jit(solution)/shard_map/all_gather | solution.py:46
  93.6 14.5 %fusion.19 = (f32[128]{0:T(128)S(1)}, f32[16384]{0:T(1024)S(1)}, f32[128,16384]{1,0:T(8,128)}) fusion(bf16[128,512]{1,0:T(8,128)(2,1)} %param.3, bf16[16384,512]{1,0:T(8,128)(2,1)} %all-gather.3.cloned.1.call-done, f32[]{:T(128)S(6)} %exp.24), kind=kOutput, calls=%fused_computation.34 | convolution fusion | flops 2153758720 | bytes 25362948 | tf_op jit(solution)/shard_map/dot_general | solution.py:52
  108.1 4.8 %exponential_reduce_fusion.1 = (f32[128]{0:T(128)S(1)}, f32[16384]{0:T(1024)S(1)}) fusion(f32[128,16384]{1,0:T(8,128)} %get-tuple-element.22, f32[128]{0:T(128)S(1)} %get-tuple-element.6, f32[16384]{0:T(1024)S(1)} %get-tuple-element.7), kind=kLoop, calls=%fused_computation.9 | loop fusion | flops 8372096 | bytes 8520704 | tf_op jit(solution)/shard_map/reduce_sum | solution.py:56
  113.7 8.2 %all-to-all-start = ((f32[128,1,256]{2,1,0:T(1,128)}), f32[128,1,256]{2,1,0:T(1,128)S(1)}, u32[]{:S(2)}, u32[]{:S(2)}) async-start(f32[128,1,256]{2,1,0:T(1,128)} %all_to_all.8), calls=%async_computation | async-start | bytes 262144 | tf_op jit(solution)/shard_map/all_to_all | solution.py:18
  121.9 0.9 constant_dynamic-slice_fusion
  122.7 1.2 gather_fusion
  125.9 5.2 %all-to-all-done = f32[128,1,256]{2,1,0:T(1,128)S(1)} async-done(((f32[128,1,256]{2,1,0:T(1,128)}), f32[128,1,256]{2,1,0:T(1,128)S(1)}, u32[]{:S(2)}, u32[]{:S(2)}) %all-to-all-start) | async-done | bytes 131104 | tf_op jit(solution)/shard_map/all_to_all | solution.py:18
  133.1 0.8 dynamic-update-slice
  133.9 50.3 %all_gather.58 = f32[16384,2]{0,1:T(2,128)S(1)} all-gather(f32[128,2]{0,1:T(2,128)S(1)} %pad_maximum_fusion.1), channel_id=1, replica_groups=mesh['dp_0'=4,'dp_1'=4,'dp_2'=2,'group'=4] {'dp_0','dp_1','dp_2','group'}, dimensions={0}, use_global_device_ids=true | all-gather | bytes 132096 | tf_op jit(solution)/shard_map/all_gather | solution.py:28
  184.2 6.5 %multiply_reduce_fusion = f32[]{:T(128)} fusion(f32[128,16384]{1,0:T(8,128)} %get-tuple-element.22, s32[128]{0:T(128)S(1)} %iota_add_fusion, f32[16384]{0:T(1024)S(1)} %bitcast.32, f32[128]{0:T(128)S(1)} %get-tuple-element.19), kind=kLoop, calls=%fused_computation.3 | loop fusion | flops 18874368 | bytes 8455172 | tf_op jit(solution)/shard_map/reduce_sum | solution.py:77
  190.7 1.4 dynamic-update-slice.4
  192.7 9.8 %all-reduce.10 = (f32[4]{0:T(128)S(1)}, f32[4]{0:T(128)S(1)}) all-reduce(f32[4]{0:T(128)S(1)} %dynamic-update-slice, f32[4]{0:T(128)S(1)} %dynamic-update-slice.4), channel_id=1, replica_groups=mesh['dp_0'=4,'dp_1'=4,'dp_2'=2,'group'=4] {'dp_0'}, use_global_device_ids=true, to_apply=%add | all-reduce | flops 8 | bytes 64
  203.8 1.4 dynamic-update-slice.1
  205.2 1.4 dynamic-update-slice.5
  207.2 8.1 %all-reduce.9 = (f32[4]{0:T(128)S(1)}, f32[4]{0:T(128)S(1)}) all-reduce(f32[4]{0:T(128)S(1)} %dynamic-update-slice.1, f32[4]{0:T(128)S(1)} %dynamic-update-slice.5), channel_id=1, replica_groups=mesh['dp_0'=4,'dp_1'=4,'dp_2'=2,'group'=4] {'dp_1'}, use_global_device_ids=true, to_apply=%add.1 | all-reduce | flops 8 | bytes 64
  216.5 1.4 dynamic-update-slice.2
  217.9 1.4 dynamic-update-slice.6
  219.9 2.4 all-reduce.11
  223.5 1.4 dynamic-update-slice.3
  224.9 1.4 dynamic-update-slice.7
  226.3 9.5 %all-reduce.8 = (f32[4]{0:T(128)S(1)}, f32[4]{0:T(128)S(1)}) all-reduce(f32[4]{0:T(128)S(1)} %dynamic-update-slice.3, f32[4]{0:T(128)S(1)} %dynamic-update-slice.7), channel_id=1, replica_groups=mesh['dp_0'=4,'dp_1'=4,'dp_2'=2,'group'=4] {'group'}, use_global_device_ids=true, to_apply=%add.3 | all-reduce | flops 8 | bytes 64
  238.3 12.4 %fusion.12 = bf16[128,512]{1,0:T(8,128)(2,1)} fusion(bf16[16384,512]{1,0:T(8,128)(2,1)} %all-gather.3.cloned.1.call-done, f32[128,16384]{1,0:T(8,128)} %get-tuple-element.22, s32[128]{0:T(128)S(1)} %iota_add_fusion, f32[16384]{0:T(1024)S(1)} %bitcast.33, f32[128]{0:T(128)S(1)} %get-tuple-element.19, f32[]{:T(128)S(6)} %exp.24), kind=kOutput, calls=%fused_computation.19 | convolution fusion | flops 2164391936 | bytes 25363460 | tf_op jit(solution)/shard_map/dot_general | solution.py:80
  250.7 18.5 %fusion.15 = bf16[128,512]{1,0:T(8,128)(2,1)} fusion(bf16[16384,512]{1,0:T(8,128)(2,1)} %all-gather.5.cloned.1.call-done, bf16[128,512]{1,0:T(8,128)(2,1)S(1)} %copy-done, s32[128]{0:T(128)S(1)} %iota_add_fusion, f32[128]{0:T(128)S(1)} %get-tuple-element.17, f32[16384]{0:T(1024)S(1)} %bitcast.35, f32[]{:T(128)S(6)} %exp.24), kind=kOutput, calls=%fused_computation.20 | convolution fusion | flops 4313972736 | bytes 17105924 | tf_op jit(solution)/shard_map/dot_general | solution.py:89
  (44 shorter events, 10.8 us)
Async XLA Ops:
  7.2 86.4 %all-gather.3.cloned.1.call-start = ((), (), s32[]{:S(2)}) async-start(), calls=%async_computation.1 | async-start | bytes 16908288 | tf_op jit(solution)/shard_map/all_gather | solution.py:46
  7.9 242.8 %all-gather.5.cloned.1.call-start = ((), (), s32[]{:S(2)}) async-start(), calls=%async_computation.2 | async-start | bytes 16908288 | tf_op jit(solution)/shard_map/all_gather | solution.py:47
  108.1 84.0 %copy-start.3 = (u32[128]{0:T(128)S(1)}, u32[128]{0:T(128)}, u32[]{:S(2)}) copy-start(u32[128]{0:T(128)} %constant.68) | copy-start | bytes 1540
  108.1 98.5 %copy-start.2 = (u32[128]{0:T(128)S(1)}, u32[128]{0:T(128)}, u32[]{:S(2)}) copy-start(u32[128]{0:T(128)} %constant.73) | copy-start | bytes 1540
  108.1 111.2 %copy-start.1 = (u32[128]{0:T(128)S(1)}, u32[128]{0:T(128)}, u32[]{:S(2)}) copy-start(u32[128]{0:T(128)} %constant.78) | copy-start | bytes 1540
  113.7 17.4 %all-to-all-start = ((f32[128,1,256]{2,1,0:T(1,128)}), f32[128,1,256]{2,1,0:T(1,128)S(1)}, u32[]{:S(2)}, u32[]{:S(2)}) async-start(f32[128,1,256]{2,1,0:T(1,128)} %all_to_all.8), calls=%async_computation | async-start | bytes 262144 | tf_op jit(solution)/shard_map/all_to_all | solution.py:18
  238.3 12.4 %copy-start = (bf16[128,512]{1,0:T(8,128)(2,1)S(1)}, bf16[128,512]{1,0:T(8,128)(2,1)}, u32[]{:S(2)}) copy-start(bf16[128,512]{1,0:T(8,128)(2,1)} %param.4) | copy-start | bytes 393220
Sparse Core Ops, SparseCore 0:
  11.1 82.4 all-gather.2
  96.7 79.4 all-gather.4
